TPU v7x, 32 devices: a whole 2x2x4 slice. The times are simulated.
32 devices in a mesh: dom: 16 (over z, y, x), tm: 2 (over core).
Axes of the slice: x: 2, y: 2, z: 4, core: 2. Of those that a mesh axis runs over, the one named last changes fastest.
Arguments:
- sources: bfloat16 [256, 3, 16, 256], P('dom', None, 'tm'), may hold values from -6 to 6
- weights: bfloat16 [48, 16, 256, 256], P('dom', None, None, 'tm'), may hold values from -0.09375 to 0.09375
- intersect: int32 [48, 16], replicated, may hold values from 0 to 255, as said below
- block_row: int32 [256], replicated, may hold values from 0 to 255, as said below
- slot_tile: int32 [48], replicated, may hold values from 0 to 47, as said below
Outputs:
- acoustic_source: bfloat16 [48, 3, 16, 256], P('dom', None, 'tm')
- source_rate: bfloat16 [48, 3, 16, 256], P('dom', None, 'tm')
Inputs may be any that keep to these rules, and one draw needn't show every extreme that they name: `intersect`: over the 48 links of the slots held by one index of dom, exactly 24 distinct source rows are named, each by exactly two links; no index of dom holds more than 2 of these rows, and some index holds exactly 2. `block_row`: A permutation of the block ids. `slot_tile`: A permutation of the tile ids.
All inputs are finite; a program needn't handle non-finite values.
Results may differ from a plain program's by a relative error of at most 0.007.
Values may be sent and summed in bfloat16 or wider, within the bound.
A program may use at most 64 MiB of HBM per device.

v0:
```python
import functools

import jax
import jax.numpy as jnp
from jax import lax
from jax.experimental import pallas as pl
from jax.experimental.pallas import tpu as pltpu
from jax.sharding import PartitionSpec as P


BIG = 1 << 30


def lookup(table, index):
    lanes = 128
    within, group = index & (lanes - 1), index >> 7
    outs = []
    for at in range(0, index.shape[1], lanes):
        value = jnp.zeros((index.shape[0], lanes), jnp.int32)
        for g in range(table.shape[1] // lanes):
            got = jnp.take_along_axis(
                table[:, g * lanes : (g + 1) * lanes],
                within[:, at : at + lanes],
                axis=1,
                mode="promise_in_bounds",
            )
            value = jnp.where(group[:, at : at + lanes] == g, got, value)
        outs.append(value)
    return outs[0] if len(outs) == 1 else jnp.concatenate(outs, axis=1)


def steps(count, body):
    if count <= 16:
        for i in range(count):
            body(i)
    else:
        def step(i, carry):
            body(i)
            return carry
        lax.fori_loop(0, count, step, 0)


def kernel(
    domains, per_owner,
    tile_hbm, row_hbm, cross_hbm, src_hbm, w_hbm, out_ref,
    tile_ref, row_ref, cross_ref, src_ref,
    wide_tile, wide_row, wide_cross, send_to, link_one, link_two,
    w_ref, pack, buf, acc, edge, beyond,
    in_sem, w_sem, send_sem, recv_sem, wsend_sem, wrecv_sem, edge_sem,
):
    me = lax.axis_index("dom")
    core = lax.axis_index("tm")
    other = 1 - core
    links, width = w_ref.shape[1], w_ref.shape[3]
    blocks, comps, half, cells = src_ref.shape
    tiles = acc.shape[0]
    link_count = links // tiles
    count = comps * half
    mesh_type = pl.DeviceIdType.MESH

    def offset(i):
        return i + 1

    barrier = pltpu.get_barrier_semaphore()

    def greet(i):
        to = lax.rem(me + i + 1, domains)
        pl.semaphore_signal(barrier, inc=1, device_id=(to, core), device_id_type=mesh_type)

    steps(domains - 1, greet)
    pl.semaphore_signal(barrier, inc=1, device_id=(me, other), device_id_type=mesh_type)

    inputs = [
        pltpu.make_async_copy(source, target, in_sem.at[i])
        for i, (source, target) in enumerate(
            (
                (cross_hbm, cross_ref),
                (tile_hbm, tile_ref),
                (row_hbm, row_ref),
                (src_hbm, src_ref),
            )
        )
    ]
    for load in inputs:
        load.start()
    parts = [pl.ds(t * link_count, link_count) for t in range(tiles)]
    loads = [
        pltpu.make_async_copy(w_hbm.at[part], w_ref.at[core, part], w_sem.at[t])
        for t, part in enumerate(parts)
    ]
    for load in loads:
        load.start()

    wide_tile[...] = jnp.zeros_like(wide_tile)
    wide_cross[...] = jnp.zeros_like(wide_cross)
    wide_row[...] = jnp.zeros_like(wide_row)
    for load in inputs[:3]:
        load.wait()
    wide_tile[:, : tile_ref.shape[1]] = jnp.broadcast_to(
        tile_ref[...], (link_count, tile_ref.shape[1])
    )
    wide_cross[:, : cross_ref.shape[1]] = cross_ref[...]
    wide_row[:, : row_ref.shape[1]] = jnp.broadcast_to(
        row_ref[...], (link_count, row_ref.shape[1])
    )
    rows = lookup(wide_row[...], lookup(wide_cross[...], wide_tile[...]))

    slots = rows.shape[1]
    lane = lax.broadcasted_iota(jnp.int32, (1, slots), 1)
    place = lax.rem(lane, tiles)
    local = rows - me * blocks
    mine = (local >= 0) & (local < blocks)
    last = jnp.full((1, slots), -1, jnp.int32)
    for j in range(per_owner):
        least = jnp.min(jnp.where(mine & (local > last), local, BIG), axis=0, keepdims=True)
        joint = least
        for t in range(1, tiles):
            joint = jnp.minimum(joint, pltpu.roll(least, slots - t, 1))
        last = joint
        for t in range(1, tiles):
            last = jnp.where(place == t, pltpu.roll(joint, t, 1), last)
        index = jnp.minimum(last, blocks - 1)
        for d in range(domains):
            send_to[d * per_owner + j] = index[0, d * tiles]

    def fill(d):
        for j in range(per_owner):
            pack[d, j] = src_ref[send_to[d * per_owner + j]]

    inputs[3].wait()
    steps(domains, fill)
    for j in range(per_owner):
        buf[me * per_owner + j] = src_ref[send_to[me * per_owner + j]]

    pl.semaphore_wait(barrier, domains)

    def exchange(to, frm):
        return pltpu.make_async_remote_copy(
            src_ref=pack.at[to],
            dst_ref=buf.at[pl.ds(frm * per_owner, per_owner)],
            send_sem=send_sem.at[to],
            recv_sem=recv_sem.at[frm],
            device_id=(to, core),
            device_id_type=mesh_type,
        )

    def send(i):
        exchange(lax.rem(me + offset(i), domains), me).start()

    steps(domains - 1, send)

    swaps = [
        pltpu.make_async_remote_copy(
            src_ref=w_ref.at[core, part],
            dst_ref=w_ref.at[core, part],
            send_sem=wsend_sem.at[t],
            recv_sem=wrecv_sem.at[t],
            device_id=(me, other),
            device_id_type=mesh_type,
        )
        for t, part in enumerate(parts)
    ]
    for load, swap in zip(loads, swaps):
        load.wait()
        swap.start()

    owners = -(-domains // 128) * 128
    around = lax.broadcasted_iota(jnp.int32, (1, owners), 1)
    owner = around + me
    owner = jnp.where(owner >= domains, owner - domains, owner)
    link = lax.broadcasted_iota(jnp.int32, (link_count, owners), 0)
    locals_ = []
    for t in range(tiles):
        column = jnp.sum(jnp.where(lane == me * tiles + t, rows, 0), axis=1, keepdims=True)
        at = column - owner * blocks
        locals_.append(jnp.where((at >= 0) & (at < blocks), at, BIG))
    last = jnp.full((1, owners), -1, jnp.int32)
    for j in range(per_owner):
        least = [jnp.where(at > last, at, BIG) for at in locals_]
        last = jnp.min(functools.reduce(jnp.minimum, least), axis=0, keepdims=True)
        one = jnp.full((link_count, owners), BIG, jnp.int32)
        two = jnp.full((link_count, owners), -1, jnp.int32)
        for t in range(tiles):
            hit = (locals_[t] == last) & (last < BIG)
            one = jnp.minimum(one, jnp.where(hit, link + t * link_count, BIG))
            two = jnp.maximum(two, jnp.where(hit, link + t * link_count, -1))
        one = jnp.min(one, axis=0, keepdims=True)
        two = jnp.max(two, axis=0, keepdims=True)
        for i in range(domains):
            link_one[i * per_owner + j] = one[0, i]
            link_two[i * per_owner + j] = two[0, i]

    acc[...] = jnp.zeros_like(acc)
    def product(i):
        frm = lax.rem(me + i, domains)
        for j in range(per_owner):
            rows_here = buf[frm * per_owner + j].astype(jnp.float32)
            lhs = rows_here.reshape(count, cells).astype(jnp.bfloat16)
            one = link_one[i * per_owner + j]
            two = link_two[i * per_owner + j]
            at_one, at_two = jnp.minimum(one, links - 1), jnp.maximum(two, 0)
            quad = jnp.concatenate(
                [w_ref[0, at_one], w_ref[1, at_one], w_ref[0, at_two], w_ref[1, at_two]], axis=1
            )
            both = jnp.dot(lhs, quad, preferred_element_type=jnp.float32)
            for t in range(tiles):
                first, end = t * link_count, (t + 1) * link_count
                acc[t] += jnp.where(
                    (one >= first) & (one < end), both[:, : 2 * width], 0.0
                ) + jnp.where((two >= first) & (two < end), both[:, 2 * width :], 0.0)

    def arrive(i):
        frm = lax.rem(me - offset(i) + domains, domains)
        incoming = pltpu.make_async_remote_copy(
            src_ref=pack.at[0],
            dst_ref=buf.at[pl.ds(frm * per_owner, per_owner)],
            send_sem=send_sem.at[frm],
            recv_sem=recv_sem.at[frm],
            device_id=(frm, core),
            device_id_type=mesh_type,
        )
        incoming.wait_recv()

    def weights_in():
        for t, part in enumerate(parts):
            pltpu.make_async_remote_copy(
                src_ref=w_hbm.at[part],
                dst_ref=w_ref.at[other, part],
                send_sem=wsend_sem.at[t],
                recv_sem=wrecv_sem.at[t],
                device_id=(me, other),
                device_id_type=mesh_type,
            ).wait_recv()

    weights_in()
    product(0)
    if domains <= 16:
        for i in range(domains - 1):
            arrive(i)
            product(domains - offset(i))
    else:
        steps(domains - 1, arrive)
        steps(domains - 1, lambda i: product(i + 1))

    total = acc[...].reshape(tiles, comps, half, 2 * width)
    edge[...] = jnp.where(core == 0, total[:, :, half - 1], total[:, :, 0])
    halo = pltpu.make_async_remote_copy(
        src_ref=edge,
        dst_ref=beyond,
        send_sem=edge_sem.at[0],
        recv_sem=edge_sem.at[1],
        device_id=(me, other),
        device_id_type=mesh_type,
    )
    out_ref[0] = total.astype(jnp.bfloat16)

    def drain(i):
        exchange(lax.rem(me + i + 1, domains), me).wait_send()

    steps(domains - 1, drain)
    for swap in swaps:
        swap.wait_send()
    halo.start()
    halo.wait()
    sample = lax.broadcasted_iota(jnp.int32, (half, 2 * width), 0)
    for t in range(tiles):
        for p in range(comps):
            here = total[t, p]
            outer = jnp.broadcast_to(beyond[t, pl.ds(p, 1)], here.shape)
            later = pltpu.roll(here, half - 1, 0)
            prior = pltpu.roll(here, 1, 0)
            later = jnp.where((sample == half - 1) & (core == 0), outer, later)
            prior = jnp.where((sample == 0) & (core == 1), outer, prior)
            rate = jnp.where(
                (sample == 0) & (core == 0),
                later - here,
                jnp.where(
                    (sample == half - 1) & (core == 1), here - prior, (later - prior) * 0.5
                ),
            )
            out_ref[1, t, p] = rate.astype(jnp.bfloat16)


def deliver(both_ref, source_ref, rate_ref):
    source_ref[...] = both_ref[0]
    rate_ref[...] = both_ref[1]


def shards(sources, weights, intersect, block_row, slot_tile):
    domains = lax.axis_size("dom")
    tiles, link_count, cells, width = weights.shape
    blocks, comps, half, _ = sources.shape
    links = tiles * link_count
    pool = links // 2
    per_owner = (pool + domains - 1) // domains
    vmem, smem = pltpu.VMEM, pltpu.SMEM
    shape = (tiles, comps, half, 2 * width)
    out = jax.ShapeDtypeStruct(shape, jnp.bfloat16)
    block = (comps, half, cells)
    dma = pltpu.SemaphoreType.DMA
    in_vmem = pl.BlockSpec(memory_space=vmem)

    def wide(n):
        return vmem((link_count, -(-n // 128) * 128), jnp.int32)

    both = pl.pallas_call(
        functools.partial(kernel, domains, per_owner),
        out_shape=jax.ShapeDtypeStruct((2,) + shape, jnp.bfloat16),
        in_specs=[pl.BlockSpec(memory_space=pl.ANY)] * 5,
        out_specs=in_vmem,
        scratch_shapes=[
            vmem((1, slot_tile.shape[0]), jnp.int32),
            vmem((1, block_row.shape[0]), jnp.int32),
            vmem((link_count, intersect.shape[0]), jnp.int32),
            vmem(sources.shape, jnp.bfloat16),
            wide(slot_tile.shape[0]),
            wide(block_row.shape[0]),
            wide(intersect.shape[0]),
            smem((domains * per_owner,), jnp.int32),
            smem((domains * per_owner,), jnp.int32),
            smem((domains * per_owner,), jnp.int32),
            vmem((2, links, cells, width), jnp.bfloat16),
            vmem((domains, per_owner) + block, jnp.bfloat16),
            vmem((domains * per_owner,) + block, jnp.bfloat16),
            vmem((tiles, comps * half, 2 * width), jnp.float32),
            vmem((tiles, comps, 2 * width), jnp.float32),
            vmem((tiles, comps, 2 * width), jnp.float32),
            dma((4,)),
            dma((tiles,)),
            dma((domains,)),
            dma((domains,)),
            dma((tiles,)),
            dma((tiles,)),
            dma((2,)),
        ],
        compiler_params=pltpu.CompilerParams(collective_id=0, has_side_effects=True),
        cost_estimate=pl.CostEstimate(
            flops=4 * comps * half * weights.size,
            bytes_accessed=2 * weights.size,
            transcendentals=0,
        ),
    )(
        slot_tile.reshape(1, -1),
        block_row.reshape(1, -1),
        intersect.T,
        sources,
        weights.reshape(links, cells, width),
    )
    return pl.pallas_call(
        deliver,
        out_shape=(out, out),
        in_specs=[in_vmem],
        out_specs=(in_vmem, in_vmem),
    )(both)


def solution(mesh):
    return jax.shard_map(
        shards,
        mesh=mesh,
        in_specs=(P("dom", None, "tm", None), P("dom", None, None, "tm"), P(), P(), P()),
        out_specs=(P("dom", None, "tm", None), P("dom", None, "tm", None)),
        check_vma=False,
    )
```

profile of v0, /device:TPU:25, one launch (start us, length us, event | category | flops | bytes accessed | tf_op | source)
XLA Modules:
  0.0 20.0 jit_solution(8449481517691092472)
XLA Ops:
  0.6 17.9 %shard_map.68.both_ref = bf16[2,3,3,8,256]{4,3,2,1,0:T(8,128)(2,1)} custom-call(s32[1,48]{1,0:T(1,128)} %bitcast.7, s32[1,256]{1,0:T(1,128)} %bitcast.6, s32[16,48]{1,0:T(8,128)} %bitcast.5, bf16[16,3,8,256]{3,2,1,0:T(8,128)(2,1)} %src_hbm.1, bf16[48,256,128]{2,1,0:T(8,128)(2,1)} %bitcast.4), custom_call_target="tpu_custom_call" | custom-call | flops 150994944 | bytes 3145728 | tf_op jit(solution)/shard_map/pallas_call | solution.py:306
  18.5 1.5 %shard_map.69 = (bf16[3,3,8,256]{3,2,1,0:T(8,128)(2,1)}, bf16[3,3,8,256]{3,2,1,0:T(8,128)(2,1)}) custom-call(bf16[2,3,3,8,256]{4,3,2,1,0:T(8,128)(2,1)} %shard_map.68.both_ref), custom_call_target="tpu_custom_call" | custom-call | tf_op jit(solution)/shard_map/pallas_call | solution.py:349
where the time goes:
time: 20.2 us; the launch traced here: 20 us
  Pallas kernels  19.4 us (96%)
  between operations  0.64 us (3%)
    pallas_call x1, Pallas kernels, shards(): pl.pallas_call(functools.partial(kernel, domains, per_owner), out_shape=j...  17.9 us
    pallas_call x1, Pallas kernels, shards(): pl.pallas_call(deliver, out_shape=(out, out), in_specs=[in_vmem], out_spe...  1.52 us

commit v1 on v0

v1 whole, which is shorter than its diff:
```python
import functools

import jax
import jax.numpy as jnp
from jax import lax
from jax.experimental import pallas as pl
from jax.experimental.pallas import tpu as pltpu
from jax.sharding import PartitionSpec as P


BIG = 1 << 30
LANES = 128


def lookup(table, index):
    within, group = index & (LANES - 1), index >> 7
    outs = []
    for at in range(0, index.shape[1], LANES):
        value = jnp.zeros((index.shape[0], LANES), jnp.int32)
        for g in range(table.shape[1] // LANES):
            got = jnp.take_along_axis(
                table[:, g * LANES : (g + 1) * LANES],
                within[:, at : at + LANES],
                axis=1,
                mode="promise_in_bounds",
            )
            value = jnp.where(group[:, at : at + LANES] == g, got, value)
        outs.append(value)
    return outs[0] if len(outs) == 1 else jnp.concatenate(outs, axis=1)


def steps(count, body):
    if count <= 16:
        for i in range(count):
            body(i)
    else:
        def step(i, carry):
            body(i)
            return carry
        lax.fori_loop(0, count, step, 0)


def kernel(
    domains, per_owner,
    tile_hbm, row_hbm, cross_hbm, src_hbm, w_hbm, out_ref,
    tile_ref, row_ref, cross_ref, src_ref,
    wide_tile, wide_row, wide_cross, send_to, link_one, link_two,
    w_ref, pack, buf, acc, edge, beyond,
    in_sem, w_sem, send_sem, recv_sem, wsend_sem, wrecv_sem, edge_sem, flag_sem, near_sem,
):
    me = lax.axis_index("dom")
    core = lax.axis_index("tm")
    other = 1 - core
    links, width = w_ref.shape[1], w_ref.shape[3]
    blocks, comps, half, cells = src_ref.shape
    tiles = acc.shape[0]
    link_count = links // tiles
    count = comps * half
    mesh_type = pl.DeviceIdType.MESH
    mid, quarter = domains // 2, domains // 4
    upper = me // mid
    lower = 1 - upper
    plane = me // quarter
    inner = (plane + 1) // 2 % 2 * quarter
    even = (1 - plane % 2) * quarter

    def key(d):
        return (1 - d // mid) * (d % 2 + d // 2 % 2 + d // 4) * domains + d

    def wait_if(condition, sem, value):
        @pl.when(condition)
        def _():
            pl.semaphore_wait(sem, value)

    def source_of(i):
        if domains == 16:
            if i < quarter:
                return me ^ i
            if i < 2 * quarter:
                return me ^ (domains - 1 - (i - quarter)) ^ inner
            if i < 3 * quarter:
                return me ^ (mid - 1 - (i - 2 * quarter))
            return me ^ (domains - 1 - quarter - (i - 3 * quarter)) ^ inner
        return me ^ i

    inputs = [
        pltpu.make_async_copy(source, target, in_sem.at[i])
        for i, (source, target) in enumerate(
            (
                (tile_hbm, tile_ref),
                (cross_hbm, cross_ref),
                (row_hbm, row_ref),
                (src_hbm, src_ref),
            )
        )
    ]
    for load in inputs:
        load.start()

    barrier = pltpu.get_barrier_semaphore()
    pl.semaphore_signal(barrier, inc=1, device_id=(me, other), device_id_type=mesh_type)

    def greet(i):
        across, near = domains - 1 - i, upper * mid + i

        @pl.when(upper == 0)
        def _():
            pl.semaphore_signal(
                barrier, inc=1, device_id=(across, core), device_id_type=mesh_type
            )

        @pl.when(key(near) > key(me))
        def _():
            pl.semaphore_signal(
                barrier, inc=1, device_id=(near, core), device_id_type=mesh_type
            )

    steps(mid, greet)

    load_w = pltpu.make_async_copy(w_hbm, w_ref.at[core], w_sem)
    load_w.start()

    wide_tile[...] = jnp.zeros_like(wide_tile)
    wide_cross[...] = jnp.zeros_like(wide_cross)
    wide_row[...] = jnp.zeros_like(wide_row)

    def swap_to(part):
        return pltpu.make_async_remote_copy(
            src_ref=w_hbm,
            dst_ref=w_ref.at[part],
            send_sem=wsend_sem,
            recv_sem=wrecv_sem,
            device_id=(me, other),
            device_id_type=mesh_type,
        )

    swap = swap_to(core)
    before = sum((key(upper * mid + i) < key(me)).astype(jnp.int32) for i in range(mid))

    def announce(i):
        near = upper * mid + i

        @pl.when(key(near) < key(me))
        def _():
            pl.semaphore_signal(near_sem, inc=1, device_id=(near, core), device_id_type=mesh_type)

        @pl.when(upper == 1)
        def _():
            pl.semaphore_signal(
                flag_sem.at[me % mid], inc=1, device_id=(i, core), device_id_type=mesh_type
            )

    @pl.when(upper == 0)
    def _():
        pl.semaphore_wait(barrier, 1 + before)
        steps(mid, announce)
        swap.start()

    for load in inputs[:3]:
        load.wait()
    wide_tile[:, : tile_ref.shape[1]] = jnp.broadcast_to(
        tile_ref[...], (link_count, tile_ref.shape[1])
    )
    wide_cross[:, : cross_ref.shape[1]] = cross_ref[...]
    wide_row[:, : row_ref.shape[1]] = jnp.broadcast_to(
        row_ref[...], (link_count, row_ref.shape[1])
    )
    owners = -(-domains // LANES) * LANES
    around = lax.broadcasted_iota(jnp.int32, (1, owners), 1)
    lane = lax.broadcasted_iota(jnp.int32, (link_count, owners), 1)
    named = lookup(wide_row[...], wide_cross[...])
    rows = []
    for t in range(tiles):
        slot = jnp.minimum(lane * tiles + t, tile_ref.shape[1] - 1)
        rows.append(lookup(named, lookup(wide_tile[...], slot)))

    base = me * blocks
    locals_ = [
        jnp.where((row >= base) & (row < base + blocks), row - base, BIG) for row in rows
    ]
    last = jnp.full((1, owners), -1, jnp.int32)
    for j in range(per_owner):
        left = [jnp.where(at > last, at, BIG) for at in locals_]
        last = jnp.min(functools.reduce(jnp.minimum, left), axis=0, keepdims=True)
        index = jnp.minimum(last, blocks - 1)
        for d in range(domains):
            send_to[d * per_owner + j] = index[0, d]

    def fill(d):
        for j in range(per_owner):
            pack[d, j] = src_ref[send_to[d * per_owner + j]]

    inputs[3].wait()
    steps(domains, fill)
    for j in range(per_owner):
        buf[me * per_owner + j] = src_ref[send_to[me * per_owner + j]]

    def exchange(to):
        return pltpu.make_async_remote_copy(
            src_ref=pack.at[to],
            dst_ref=buf.at[pl.ds(me * per_owner, per_owner)],
            send_sem=send_sem,
            recv_sem=recv_sem.at[me],
            device_id=(to, core),
            device_id_type=mesh_type,
        )

    def first(i):
        to = me ^ (domains - 1 - i) ^ even ^ (lower * (quarter - 1))
        wait_if(upper == 0, flag_sem.at[to % mid], 1)
        exchange(to).start()

    def second(i):
        to = me ^ (mid + quarter - 1 - i) ^ even
        wait_if(upper == 0, flag_sem.at[to % mid], 1)
        exchange(to).start()

    @pl.when(upper == 1)
    def _():
        pl.semaphore_wait(barrier, mid + 1 + before)
        steps(mid, announce)
        steps(quarter, first)
        steps(quarter, second)
        swap.start()

    wait_if(before < mid - 1, near_sem, mid - 1 - before)
    steps(mid - 1, lambda i: exchange(me ^ (mid - 1 - i)).start())

    @pl.when(upper == 0)
    def _():
        steps(quarter, first)
        steps(quarter, second)

    link = lax.broadcasted_iota(jnp.int32, (link_count, owners), 0)
    mine = []
    for t in range(tiles):
        column = jnp.sum(jnp.where(lane == me, rows[t], 0), axis=1, keepdims=True)
        at = column - around * blocks
        mine.append(jnp.where((at >= 0) & (at < blocks), at, BIG))
    last = jnp.full((1, owners), -1, jnp.int32)
    for j in range(per_owner):
        least = [jnp.where(at > last, at, BIG) for at in mine]
        last = jnp.min(functools.reduce(jnp.minimum, least), axis=0, keepdims=True)
        one = jnp.full((link_count, owners), BIG, jnp.int32)
        two = jnp.full((link_count, owners), -1, jnp.int32)
        for t in range(tiles):
            hit = (mine[t] == last) & (last < BIG)
            one = jnp.minimum(one, jnp.where(hit, link + t * link_count, BIG))
            two = jnp.maximum(two, jnp.where(hit, link + t * link_count, -1))
        one = jnp.min(one, axis=0, keepdims=True)
        two = jnp.max(two, axis=0, keepdims=True)
        for i in range(domains):
            link_one[i * per_owner + j] = one[0, i]
            link_two[i * per_owner + j] = two[0, i]

    acc[...] = jnp.zeros_like(acc)

    def product(i):
        frm = source_of(i)
        for j in range(per_owner):
            rows_here = buf[frm * per_owner + j].astype(jnp.float32)
            lhs = rows_here.reshape(count, cells).astype(jnp.bfloat16)
            one = link_one[frm * per_owner + j]
            two = link_two[frm * per_owner + j]
            at_one, at_two = jnp.minimum(one, links - 1), jnp.maximum(two, 0)
            quad = jnp.concatenate(
                [w_ref[0, at_one], w_ref[1, at_one], w_ref[0, at_two], w_ref[1, at_two]], axis=1
            )
            both = jnp.dot(lhs, quad, preferred_element_type=jnp.float32)
            for t in range(tiles):
                first, end = t * link_count, (t + 1) * link_count
                acc[t] += jnp.where(
                    (one >= first) & (one < end), both[:, : 2 * width], 0.0
                ) + jnp.where((two >= first) & (two < end), both[:, 2 * width :], 0.0)

    def arrive(i):
        frm = source_of(i)
        pltpu.make_async_remote_copy(
            src_ref=pack.at[0],
            dst_ref=buf.at[pl.ds(frm * per_owner, per_owner)],
            send_sem=send_sem,
            recv_sem=recv_sem.at[frm],
            device_id=(frm, core),
            device_id_type=mesh_type,
        ).wait_recv()

    load_w.wait()
    swap_to(other).wait_recv()

    product(0)

    def take(i):
        arrive(i + 1)
        product(i + 1)

    steps(domains - 1, take)

    total = acc[...].reshape(tiles, comps, half, 2 * width)
    edge[...] = jnp.where(core == 0, total[:, :, half - 1], total[:, :, 0])
    halo = pltpu.make_async_remote_copy(
        src_ref=edge,
        dst_ref=beyond,
        send_sem=edge_sem.at[0],
        recv_sem=edge_sem.at[1],
        device_id=(me, other),
        device_id_type=mesh_type,
    )
    out_ref[0] = total.astype(jnp.bfloat16)

    sent = pack.at[pl.ds(0, domains - 1)]
    pltpu.make_async_remote_copy(
        src_ref=sent,
        dst_ref=sent,
        send_sem=send_sem,
        recv_sem=recv_sem.at[me],
        device_id=(me, other),
        device_id_type=mesh_type,
    ).wait_send()
    swap.wait_send()
    halo.start()
    halo.wait()
    sample = lax.broadcasted_iota(jnp.int32, (half, 2 * width), 0)
    for t in range(tiles):
        for p in range(comps):
            now = total[t, p]
            outer = jnp.broadcast_to(beyond[t, pl.ds(p, 1)], now.shape)
            later = pltpu.roll(now, half - 1, 0)
            prior = pltpu.roll(now, 1, 0)
            later = jnp.where((sample == half - 1) & (core == 0), outer, later)
            prior = jnp.where((sample == 0) & (core == 1), outer, prior)
            rate = jnp.where(
                (sample == 0) & (core == 0),
                later - now,
                jnp.where(
                    (sample == half - 1) & (core == 1), now - prior, (later - prior) * 0.5
                ),
            )
            out_ref[1, t, p] = rate.astype(jnp.bfloat16)


def deliver(both_ref, source_ref, rate_ref, sem):
    copies = [
        pltpu.make_async_copy(both_ref.at[i], out, sem.at[i])
        for i, out in enumerate((source_ref, rate_ref))
    ]
    for copy in copies:
        copy.start()
    for copy in copies:
        copy.wait()


def shards(sources, weights, intersect, block_row, slot_tile):
    domains = lax.axis_size("dom")
    tiles, link_count, cells, width = weights.shape
    blocks, comps, half, _ = sources.shape
    links = tiles * link_count
    pool = links // 2
    per_owner = (pool + domains - 1) // domains
    vmem, smem = pltpu.VMEM, pltpu.SMEM
    shape = (tiles, comps, half, 2 * width)
    out = jax.ShapeDtypeStruct(shape, jnp.bfloat16)
    block = (comps, half, cells)
    dma, regular = pltpu.SemaphoreType.DMA, pltpu.SemaphoreType.REGULAR
    in_vmem = pl.BlockSpec(memory_space=vmem)
    anywhere = pl.BlockSpec(memory_space=pl.ANY)

    def wide(n):
        return vmem((link_count, -(-n // LANES) * LANES), jnp.int32)

    both = pl.pallas_call(
        functools.partial(kernel, domains, per_owner),
        out_shape=vmem((2,) + shape, jnp.bfloat16),
        in_specs=[anywhere] * 5,
        out_specs=in_vmem,
        scratch_shapes=[
            vmem((1, slot_tile.shape[0]), jnp.int32),
            vmem((1, block_row.shape[0]), jnp.int32),
            vmem((link_count, intersect.shape[0]), jnp.int32),
            vmem(sources.shape, jnp.bfloat16),
            wide(slot_tile.shape[0]),
            wide(block_row.shape[0]),
            wide(intersect.shape[0]),
            smem((domains * per_owner,), jnp.int32),
            smem((domains * per_owner,), jnp.int32),
            smem((domains * per_owner,), jnp.int32),
            vmem((2, links, cells, width), jnp.bfloat16),
            vmem((domains, per_owner) + block, jnp.bfloat16),
            vmem((domains * per_owner,) + block, jnp.bfloat16),
            vmem((tiles, comps * half, 2 * width), jnp.float32),
            vmem((tiles, comps, 2 * width), jnp.float32),
            vmem((tiles, comps, 2 * width), jnp.float32),
            dma((4,)),
            dma,
            dma,
            dma((domains,)),
            dma,
            dma,
            dma((2,)),
            regular((domains // 2,)),
            regular,
        ],
        compiler_params=pltpu.CompilerParams(collective_id=0, has_side_effects=True),
        cost_estimate=pl.CostEstimate(
            flops=4 * comps * half * weights.size,
            bytes_accessed=2 * weights.size,
            transcendentals=0,
        ),
    )(
        slot_tile.reshape(1, -1),
        block_row.reshape(1, -1),
        intersect.T,
        sources,
        weights.reshape(links, cells, width),
    )
    return pl.pallas_call(
        deliver,
        out_shape=(out, out),
        in_specs=[in_vmem],
        out_specs=(anywhere, anywhere),
        scratch_shapes=[dma((2,))],
    )(pltpu.with_memory_space_constraint(both, vmem))


def solution(mesh):
    return jax.shard_map(
        shards,
        mesh=mesh,
        in_specs=(P("dom", None, "tm", None), P("dom", None, None, "tm"), P(), P(), P()),
        out_specs=(P("dom", None, "tm", None), P("dom", None, "tm", None)),
        check_vma=False,
    )
```

time: 20.2 us -> 17.3 us (0.86)
  Pallas kernels: 19.4 us -> 16.4 us
    pallas_call x1, Pallas kernels: 17.9 us -> 15.8 us  [shards(): pl.pallas_call(functools.partial(kernel, domains, per_owner), out_shape=v...]
    pallas_call x1, Pallas kernels: 1.52 us -> 0.65 us  [shards(): pl.pallas_call(deliver, out_shape=(out, out), in_specs=[in_vmem], out_spe...]
where the time goes in v1:
time: 17.3 us; the launch traced here: 17.1 us
  Pallas kernels  16.4 us (95%)
  between operations  0.64 us (4%)
    pallas_call x1, Pallas kernels, shards(): pl.pallas_call(functools.partial(kernel, domains, per_owner), out_shape=v...  15.8 us
    pallas_call x1, Pallas kernels, shards(): pl.pallas_call(deliver, out_shape=(out, out), in_specs=[in_vmem], out_spe...  0.65 us

profile of v1, /device:TPU:25, one launch (start us, length us, event | category | flops | bytes accessed | tf_op | source)
XLA Modules:
  0.0 17.1 jit_solution(15999882776679631406)
XLA Ops:
  0.6 15.8 %shard_map.68.both_ref = bf16[2,3,3,8,256]{4,3,2,1,0:T(8,128)(2,1)S(1)} custom-call(s32[1,48]{1,0:T(1,128)} %bitcast.7, s32[1,256]{1,0:T(1,128)} %bitcast.6, s32[16,48]{1,0:T(8,128)} %bitcast.5, bf16[16,3,8,256]{3,2,1,0:T(8,128)(2,1)} %src_hbm.1, bf16[48,256,128]{2,1,0:T(8,128)(2,1)} %bitcast.4), custom_call_target="tpu_custom_call" | custom-call | flops 150994944 | bytes 3145728 | tf_op jit(solution)/shard_map/pallas_call | solution.py:370
  16.4 0.6 %shard_map.69 = (bf16[3,3,8,256]{3,2,1,0:T(8,128)(2,1)}, bf16[3,3,8,256]{3,2,1,0:T(8,128)(2,1)}) custom-call(bf16[2,3,3,8,256]{4,3,2,1,0:T(8,128)(2,1)S(1)} %shard_map.68.both_ref), custom_call_target="tpu_custom_call" | custom-call | tf_op jit(solution)/shard_map/pallas_call | solution.py:415

commit v2 on v1

--- a/solution.py
+++ b/solution.py
@@ -45,8 +45,9 @@
     tile_hbm, row_hbm, cross_hbm, src_hbm, w_hbm, out_ref,
     tile_ref, row_ref, cross_ref, src_ref,
     wide_tile, wide_row, wide_cross, send_to, link_one, link_two,
-    w_ref, pack, buf, acc, edge, beyond,
+    w_ref, pack, buf, acc, edge, beyond, twin_ref, rim_acc,
     in_sem, w_sem, send_sem, recv_sem, wsend_sem, wrecv_sem, edge_sem, flag_sem, near_sem,
+    twin_sem,
 ):
     me = lax.axis_index("dom")
     core = lax.axis_index("tm")
@@ -56,6 +57,8 @@
     tiles = acc.shape[0]
     link_count = links // tiles
     count = comps * half
+    full = per_owner * comps
+    planes = full + 1
     mesh_type = pl.DeviceIdType.MESH
     mid, quarter = domains // 2, domains // 4
     upper = me // mid
@@ -72,16 +75,10 @@
         def _():
             pl.semaphore_wait(sem, value)
 
-    def source_of(i):
-        if domains == 16:
-            if i < quarter:
-                return me ^ i
-            if i < 2 * quarter:
-                return me ^ (domains - 1 - (i - quarter)) ^ inner
-            if i < 3 * quarter:
-                return me ^ (mid - 1 - (i - 2 * quarter))
-            return me ^ (domains - 1 - quarter - (i - 3 * quarter)) ^ inner
-        return me ^ i
+    near_from = inner // quarter
+
+    def mailbox(offset):
+        return 2 + near_from * (1 + offset)
 
     inputs = [
         pltpu.make_async_copy(source, target, in_sem.at[i])
@@ -135,6 +132,16 @@
         )
 
     swap = swap_to(core)
+    twin = pltpu.make_async_remote_copy(
+        src_ref=src_hbm,
+        dst_ref=twin_ref,
+        send_sem=twin_sem.at[0],
+        recv_sem=twin_sem.at[1],
+        device_id=(me, other),
+        device_id_type=mesh_type,
+    )
+    gives = (core == 0) & (near_from == 1)
+    takes = (core == 1) & (near_from == 1)
     before = sum((key(upper * mid + i) < key(me)).astype(jnp.int32) for i in range(mid))
 
     def announce(i):
@@ -154,6 +161,7 @@
     def _():
         pl.semaphore_wait(barrier, 1 + before)
         steps(mid, announce)
+        pl.when(gives)(twin.start)
         swap.start()
 
     for load in inputs[:3]:
@@ -188,48 +196,98 @@
 
     def fill(d):
         for j in range(per_owner):
-            pack[d, j] = src_ref[send_to[d * per_owner + j]]
+            pack[pl.ds(d * planes + j * comps, comps)] = src_ref[send_to[d * per_owner + j]]
 
     inputs[3].wait()
     steps(domains, fill)
     for j in range(per_owner):
-        buf[me * per_owner + j] = src_ref[send_to[me * per_owner + j]]
-
-    def exchange(to):
+        buf[pl.ds(me * planes + j * comps, comps)] = src_ref[send_to[me * per_owner + j]]
+
+    def exchange(to, box, start=0, number=full):
         return pltpu.make_async_remote_copy(
-            src_ref=pack.at[to],
-            dst_ref=buf.at[pl.ds(me * per_owner, per_owner)],
+            src_ref=pack.at[pl.ds(to * planes + start, number)],
+            dst_ref=buf.at[pl.ds(me * planes + start, number)],
             send_sem=send_sem,
-            recv_sem=recv_sem.at[me],
+            recv_sem=recv_sem.at[box],
             device_id=(to, core),
             device_id_type=mesh_type,
         )
 
+    def across(to, **part):
+        exchange(to, mailbox((me ^ to) % quarter), **part).start()
+
+    def ready(to):
+        wait_if(upper == 0, flag_sem.at[to % mid], 1)
+
+    def first_of(i):
+        to = me ^ (domains - 1 - i) ^ even ^ (lower * (quarter - 1))
+        return jnp.where(plane == 2, i, to)
+
     def first(i):
-        to = me ^ (domains - 1 - i) ^ even ^ (lower * (quarter - 1))
-        wait_if(upper == 0, flag_sem.at[to % mid], 1)
-        exchange(to).start()
-
-    def second(i):
+        to = first_of(i)
+        ready(to)
+        across(to)
+
+    def second(i, number=full):
         to = me ^ (mid + quarter - 1 - i) ^ even
-        wait_if(upper == 0, flag_sem.at[to % mid], 1)
-        exchange(to).start()
+        ready(to)
+        across(to, number=number)
+
+    def beside(known):
+        def send(i):
+            r = mid - 1 - i
+            to = me ^ r
+
+            @pl.when((key(to) < key(me)) == known)
+            def _():
+                exchange(to, r // quarter).start()
+
+        if domains <= 16:
+            steps(mid - 1, send)
+        else:
+            steps(quarter, send)
+            steps(quarter - 1, lambda i: send(i + quarter))
 
     @pl.when(upper == 1)
     def _():
         pl.semaphore_wait(barrier, mid + 1 + before)
         steps(mid, announce)
         steps(quarter, first)
-        steps(quarter, second)
+
+        @pl.when(jnp.logical_not(takes))
+        def _():
+            steps(quarter, second)
+
+        pl.when(gives)(twin.start)
         swap.start()
 
+    beside(True)
     wait_if(before < mid - 1, near_sem, mid - 1 - before)
-    steps(mid - 1, lambda i: exchange(me ^ (mid - 1 - i)).start())
+    beside(False)
 
     @pl.when(upper == 0)
     def _():
         steps(quarter, first)
-        steps(quarter, second)
+
+        @pl.when(jnp.logical_not(takes))
+        def _():
+            steps(quarter, second)
+
+    def rim_of(i):
+        to, lines = lower * mid + i, []
+        for j in range(per_owner):
+            block = twin_ref[send_to[to * per_owner + j]].astype(jnp.float32)
+            lines.append(block[:, half - 1])
+        if half > full:
+            lines.append(jnp.zeros((half - full, cells), jnp.float32))
+        pack[to * planes + full] = jnp.concatenate(lines, axis=0).astype(jnp.bfloat16)
+
+    @pl.when(takes)
+    def _():
+        twin.wait_recv()
+        steps(mid, rim_of)
+        steps(quarter, lambda i: across(first_of(i), start=full, number=1))
+        steps(quarter, lambda i: second(i, planes))
 
     link = lax.broadcasted_iota(jnp.int32, (link_count, owners), 0)
     mine = []
@@ -255,48 +313,69 @@
 
     acc[...] = jnp.zeros_like(acc)
 
-    def product(i):
-        frm = source_of(i)
-        for j in range(per_owner):
-            rows_here = buf[frm * per_owner + j].astype(jnp.float32)
-            lhs = rows_here.reshape(count, cells).astype(jnp.bfloat16)
-            one = link_one[frm * per_owner + j]
-            two = link_two[frm * per_owner + j]
-            at_one, at_two = jnp.minimum(one, links - 1), jnp.maximum(two, 0)
-            quad = jnp.concatenate(
-                [w_ref[0, at_one], w_ref[1, at_one], w_ref[0, at_two], w_ref[1, at_two]], axis=1
-            )
-            both = jnp.dot(lhs, quad, preferred_element_type=jnp.float32)
-            for t in range(tiles):
-                first, end = t * link_count, (t + 1) * link_count
-                acc[t] += jnp.where(
-                    (one >= first) & (one < end), both[:, : 2 * width], 0.0
-                ) + jnp.where((two >= first) & (two < end), both[:, 2 * width :], 0.0)
-
-    def arrive(i):
-        frm = source_of(i)
+    def product(sources, rimmed=False):
+        totals = [acc[t] for t in range(tiles)]
+        outer = [[0.0] * tiles for _ in range(per_owner)]
+        for frm in sources:
+            for j in range(per_owner):
+                here = buf[pl.ds(frm * planes + j * comps, comps)].astype(jnp.float32)
+                lhs = here.reshape(count, cells)
+                if rimmed:
+                    rim = jnp.where(core == 1, buf[frm * planes + full].astype(jnp.float32), 0.0)
+                    lhs = jnp.concatenate([lhs, rim], axis=0)
+                lhs = lhs.astype(jnp.bfloat16)
+                one = link_one[frm * per_owner + j]
+                two = link_two[frm * per_owner + j]
+                at_one, at_two = jnp.minimum(one, links - 1), jnp.maximum(two, 0)
+                quad = jnp.concatenate(
+                    [w_ref[0, at_one], w_ref[1, at_one], w_ref[0, at_two], w_ref[1, at_two]],
+                    axis=1,
+                )
+                both = jnp.dot(lhs, quad, preferred_element_type=jnp.float32)
+                for t in range(tiles):
+                    begin, end = t * link_count, (t + 1) * link_count
+                    part = jnp.where(
+                        (one >= begin) & (one < end), both[:, : 2 * width], 0.0
+                    ) + jnp.where((two >= begin) & (two < end), both[:, 2 * width :], 0.0)
+                    totals[t] += part[:count]
+                    if rimmed:
+                        outer[j][t] += part[count:]
+        for t in range(tiles):
+            acc[t] = totals[t]
+            if rimmed:
+                parts = [outer[j][t][j * comps : (j + 1) * comps] for j in range(per_owner)]
+                rim_acc[t] += sum(parts)
+
+    def arrive(box, number):
+        rows_in = buf.at[pl.ds(0, number)]
         pltpu.make_async_remote_copy(
-            src_ref=pack.at[0],
-            dst_ref=buf.at[pl.ds(frm * per_owner, per_owner)],
+            src_ref=rows_in,
+            dst_ref=rows_in,
             send_sem=send_sem,
-            recv_sem=recv_sem.at[frm],
-            device_id=(frm, core),
+            recv_sem=recv_sem.at[box],
+            device_id=(me, other),
             device_id_type=mesh_type,
         ).wait_recv()
 
+    def beyond_mid(i, apart):
+        return me ^ (mid + i) ^ (quarter * apart)
+
     load_w.wait()
     swap_to(other).wait_recv()
 
-    product(0)
-
-    def take(i):
-        arrive(i + 1)
-        product(i + 1)
-
-    steps(domains - 1, take)
-
-    total = acc[...].reshape(tiles, comps, half, 2 * width)
-    edge[...] = jnp.where(core == 0, total[:, :, half - 1], total[:, :, 0])
+    far, near = 1 - near_from, near_from
+    outmost = jnp.where(plane == 0, 1, 0)
+
+    def own_half(i):
+        return me ^ (quarter + i)
+
+    def far_half(i):
+        return beyond_mid(i, far)
+
+    def near_half(i):
+        return beyond_mid(i, near)
+
+    rim_acc[...] = jnp.zeros_like(rim_acc)
     halo = pltpu.make_async_remote_copy(
         src_ref=edge,
         dst_ref=beyond,
@@ -305,25 +384,79 @@
         device_id=(me, other),
         device_id_type=mesh_type,
     )
+
+    def early_edge():
+        now = acc[...].reshape(tiles, comps, half, 2 * width)
+        edge[...] = now[:, :, half - 1]
+        halo.start()
+
+    if domains <= 16:
+        product([me])
+        arrive(0, (quarter - 1) * full)
+        product([me ^ r for r in range(1, quarter)])
+        arrive(1 + outmost, quarter * full)
+        product([jnp.where(plane == 0, far_half(i), own_half(i)) for i in range(quarter)])
+        arrive(2 - outmost, quarter * full)
+        product([jnp.where(plane == 0, own_half(i), far_half(i)) for i in range(quarter)])
+        pl.when(core == 0)(early_edge)
+    else:
+        arrive(0, (quarter - 1) * full)
+        arrive(1, quarter * full)
+        arrive(2, quarter * full)
+        steps(mid, lambda r: product([me ^ r]))
+        steps(quarter, lambda i: product([far_half(i)]))
+        pl.when(core == 0)(early_edge)
+
+    @pl.when(core == 0)
+    def _():
+        steps(quarter, lambda i: arrive(3 + i, full))
+
+    @pl.when(core == 1)
+    def _():
+        steps(quarter, lambda i: arrive(3 + i, planes))
+
+    if domains <= 16:
+        product([near_half(i) for i in range(quarter)], rimmed=True)
+    else:
+        steps(quarter, lambda i: product([near_half(i)], rimmed=True))
+
+    total = acc[...].reshape(tiles, comps, half, 2 * width)
+
+    @pl.when(core == 1)
+    def _():
+        edge[...] = total[:, :, 0]
+        halo.start()
+
     out_ref[0] = total.astype(jnp.bfloat16)
 
-    sent = pack.at[pl.ds(0, domains - 1)]
-    pltpu.make_async_remote_copy(
-        src_ref=sent,
-        dst_ref=sent,
-        send_sem=send_sem,
-        recv_sem=recv_sem.at[me],
-        device_id=(me, other),
-        device_id_type=mesh_type,
-    ).wait_send()
+    def drain(number):
+        sent = pack.at[pl.ds(0, number)]
+        pltpu.make_async_remote_copy(
+            src_ref=sent,
+            dst_ref=sent,
+            send_sem=send_sem,
+            recv_sem=recv_sem.at[0],
+            device_id=(me, other),
+            device_id_type=mesh_type,
+        ).wait_send()
+
+    @pl.when(takes)
+    def _():
+        drain((domains - 1) * full + mid)
+
+    @pl.when(jnp.logical_not(takes))
+    def _():
+        drain((domains - 1) * full)
+
     swap.wait_send()
-    halo.start()
-    halo.wait()
+    pl.when(gives)(twin.wait_send)
+    halo.wait_recv()
     sample = lax.broadcasted_iota(jnp.int32, (half, 2 * width), 0)
     for t in range(tiles):
+        past = beyond[t] + rim_acc[t]
         for p in range(comps):
             now = total[t, p]
-            outer = jnp.broadcast_to(beyond[t, pl.ds(p, 1)], now.shape)
+            outer = jnp.broadcast_to(past[p : p + 1], now.shape)
             later = pltpu.roll(now, half - 1, 0)
             prior = pltpu.roll(now, 1, 0)
             later = jnp.where((sample == half - 1) & (core == 0), outer, later)
@@ -336,6 +469,7 @@
                 ),
             )
             out_ref[1, t, p] = rate.astype(jnp.bfloat16)
+    halo.wait_send()
 
 
 def deliver(both_ref, source_ref, rate_ref, sem):
@@ -359,7 +493,8 @@
     vmem, smem = pltpu.VMEM, pltpu.SMEM
     shape = (tiles, comps, half, 2 * width)
     out = jax.ShapeDtypeStruct(shape, jnp.bfloat16)
-    block = (comps, half, cells)
+    block = (half, cells)
+    planes = per_owner * comps + 1
     dma, regular = pltpu.SemaphoreType.DMA, pltpu.SemaphoreType.REGULAR
     in_vmem = pl.BlockSpec(memory_space=vmem)
     anywhere = pl.BlockSpec(memory_space=pl.ANY)
@@ -384,20 +519,23 @@
             smem((domains * per_owner,), jnp.int32),
             smem((domains * per_owner,), jnp.int32),
             vmem((2, links, cells, width), jnp.bfloat16),
-            vmem((domains, per_owner) + block, jnp.bfloat16),
-            vmem((domains * per_owner,) + block, jnp.bfloat16),
+            vmem((domains * planes,) + block, jnp.bfloat16),
+            vmem((domains * planes,) + block, jnp.bfloat16),
             vmem((tiles, comps * half, 2 * width), jnp.float32),
             vmem((tiles, comps, 2 * width), jnp.float32),
+            vmem((tiles, comps, 2 * width), jnp.float32),
+            vmem(sources.shape, jnp.bfloat16),
             vmem((tiles, comps, 2 * width), jnp.float32),
             dma((4,)),
             dma,
             dma,
-            dma((domains,)),
+            dma((3 + domains // 4,)),
             dma,
             dma,
             dma((2,)),
             regular((domains // 2,)),
             regular,
+            dma((2,)),
         ],
         compiler_params=pltpu.CompilerParams(collective_id=0, has_side_effects=True),
         cost_estimate=pl.CostEstimate(

time: 17.3 us -> 16.2 us (0.936)
  Pallas kernels: 16.4 us -> 15.4 us
    pallas_call x1, Pallas kernels: 15.8 us -> 14.8 us  [shards(): pl.pallas_call(functools.partial(kernel, domains, per_owner), out_shape=v...]
where the time goes in v2:
time: 16.2 us; the launch traced here: 16.1 us
  Pallas kernels  15.4 us (95%)
  between operations  0.64 us (4%)
    pallas_call x1, Pallas kernels, shards(): pl.pallas_call(functools.partial(kernel, domains, per_owner), out_shape=v...  14.8 us
    pallas_call x1, Pallas kernels, shards(): pl.pallas_call(deliver, out_shape=(out, out), in_specs=[in_vmem], out_spe...  0.65 us

profile of v2, /device:TPU:25, one launch (start us, length us, event | category | flops | bytes accessed | tf_op | source)
XLA Modules:
  0.0 16.1 jit_solution(6526950028262354133)
XLA Ops:
  0.6 14.8 %shard_map.68.both_ref = bf16[2,3,3,8,256]{4,3,2,1,0:T(8,128)(2,1)S(1)} custom-call(s32[1,48]{1,0:T(1,128)} %bitcast.7, s32[1,256]{1,0:T(1,128)} %bitcast.6, s32[16,48]{1,0:T(8,128)} %bitcast.5, bf16[16,3,8,256]{3,2,1,0:T(8,128)(2,1)} %src_hbm.1, bf16[48,256,128]{2,1,0:T(8,128)(2,1)} %bitcast.4), custom_call_target="tpu_custom_call" | custom-call | flops 150994944 | bytes 3145728 | tf_op jit(solution)/shard_map/pallas_call | solution.py:505
  15.4 0.6 %shard_map.69 = (bf16[3,3,8,256]{3,2,1,0:T(8,128)(2,1)}, bf16[3,3,8,256]{3,2,1,0:T(8,128)(2,1)}) custom-call(bf16[2,3,3,8,256]{4,3,2,1,0:T(8,128)(2,1)S(1)} %shard_map.68.both_ref), custom_call_target="tpu_custom_call" | custom-call | tf_op jit(solution)/shard_map/pallas_call | solution.py:553

commit v3 on v2

--- a/solution.py
+++ b/solution.py
@@ -68,7 +68,8 @@
     even = (1 - plane % 2) * quarter
 
     def key(d):
-        return (1 - d // mid) * (d % 2 + d // 2 % 2 + d // 4) * domains + d
+        hops = d % 2 + d // 2 % 2 + d // quarter
+        return (4 * hops - ((d // quarter - 1) % 4 == 1)) * domains + d
 
     def wait_if(condition, sem, value):
         @pl.when(condition)
@@ -98,21 +99,13 @@
     pl.semaphore_signal(barrier, inc=1, device_id=(me, other), device_id_type=mesh_type)
 
     def greet(i):
-        across, near = domains - 1 - i, upper * mid + i
-
-        @pl.when(upper == 0)
+        to = domains - 1 - i
+
+        @pl.when(key(to) > key(me))
         def _():
-            pl.semaphore_signal(
-                barrier, inc=1, device_id=(across, core), device_id_type=mesh_type
-            )
-
-        @pl.when(key(near) > key(me))
-        def _():
-            pl.semaphore_signal(
-                barrier, inc=1, device_id=(near, core), device_id_type=mesh_type
-            )
-
-    steps(mid, greet)
+            pl.semaphore_signal(barrier, inc=1, device_id=(to, core), device_id_type=mesh_type)
+
+    steps(domains, greet)
 
     load_w = pltpu.make_async_copy(w_hbm, w_ref.at[core], w_sem)
     load_w.start()
@@ -142,27 +135,23 @@
     )
     gives = (core == 0) & (near_from == 1)
     takes = (core == 1) & (near_from == 1)
-    before = sum((key(upper * mid + i) < key(me)).astype(jnp.int32) for i in range(mid))
+    def below(start, number):
+        return sum((key(start + i) < key(me)).astype(jnp.int32) for i in range(number))
+
+    before, near_before = below(0, domains), below(upper * mid, mid)
 
     def announce(i):
-        near = upper * mid + i
-
-        @pl.when(key(near) < key(me))
+        known = key(i) < key(me)
+
+        @pl.when(known & (i // mid == upper))
         def _():
-            pl.semaphore_signal(near_sem, inc=1, device_id=(near, core), device_id_type=mesh_type)
-
-        @pl.when(upper == 1)
+            pl.semaphore_signal(near_sem, inc=1, device_id=(i, core), device_id_type=mesh_type)
+
+        @pl.when(known & (i // mid != upper))
         def _():
             pl.semaphore_signal(
                 flag_sem.at[me % mid], inc=1, device_id=(i, core), device_id_type=mesh_type
             )
-
-    @pl.when(upper == 0)
-    def _():
-        pl.semaphore_wait(barrier, 1 + before)
-        steps(mid, announce)
-        pl.when(gives)(twin.start)
-        swap.start()
 
     for load in inputs[:3]:
         load.wait()
@@ -217,11 +206,11 @@
         exchange(to, mailbox((me ^ to) % quarter), **part).start()
 
     def ready(to):
-        wait_if(upper == 0, flag_sem.at[to % mid], 1)
+        wait_if(key(to) > key(me), flag_sem.at[to % mid], 1)
 
     def first_of(i):
-        to = me ^ (domains - 1 - i) ^ even ^ (lower * (quarter - 1))
-        return jnp.where(plane == 2, i, to)
+        to = me ^ (domains - 1 - i) ^ even
+        return jnp.where(plane == 3, to, lower * mid + i)
 
     def first(i):
         to = first_of(i)
@@ -248,30 +237,27 @@
             steps(quarter, send)
             steps(quarter - 1, lambda i: send(i + quarter))
 
+    pl.semaphore_wait(barrier, 1 + before)
+    steps(domains, announce)
+    pl.when(gives)(twin.start)
+    swap.start()
+    pl.when(upper == 0)(lambda: beside(True))
+    steps(quarter, first)
+
     @pl.when(upper == 1)
     def _():
-        pl.semaphore_wait(barrier, mid + 1 + before)
-        steps(mid, announce)
-        steps(quarter, first)
-
         @pl.when(jnp.logical_not(takes))
         def _():
             steps(quarter, second)
 
-        pl.when(gives)(twin.start)
-        swap.start()
-
-    beside(True)
-    wait_if(before < mid - 1, near_sem, mid - 1 - before)
+        beside(True)
+
+    wait_if(near_before < mid - 1, near_sem, mid - 1 - near_before)
     beside(False)
 
-    @pl.when(upper == 0)
-    def _():
-        steps(quarter, first)
-
-        @pl.when(jnp.logical_not(takes))
-        def _():
-            steps(quarter, second)
+    @pl.when((upper == 0) & jnp.logical_not(takes))
+    def _():
+        steps(quarter, second)
 
     def rim_of(i):
         to, lines = lower * mid + i, []

time: 16.2 us -> 15.9 us (0.981)
  Pallas kernels: 15.4 us -> 15.1 us
    pallas_call x1, Pallas kernels: 14.8 us -> 14.5 us  [shards(): pl.pallas_call(functools.partial(kernel, domains, per_owner), out_shape=v...]
where the time goes in v3:
time: 15.9 us; the launch traced here: 15.8 us
  Pallas kernels  15.1 us (95%)
  between operations  0.64 us (4%)
    pallas_call x1, Pallas kernels, shards(): pl.pallas_call(functools.partial(kernel, domains, per_owner), out_shape=v...  14.5 us
    pallas_call x1, Pallas kernels, shards(): pl.pallas_call(deliver, out_shape=(out, out), in_specs=[in_vmem], out_spe...  0.65 us

profile of v3, /device:TPU:25, one launch (start us, length us, event | category | flops | bytes accessed | tf_op | source)
XLA Modules:
  0.0 15.8 jit_solution(12512896039003805866)
XLA Ops:
  0.6 14.5 %shard_map.68.both_ref = bf16[2,3,3,8,256]{4,3,2,1,0:T(8,128)(2,1)S(1)} custom-call(s32[1,48]{1,0:T(1,128)} %bitcast.7, s32[1,256]{1,0:T(1,128)} %bitcast.6, s32[16,48]{1,0:T(8,128)} %bitcast.5, bf16[16,3,8,256]{3,2,1,0:T(8,128)(2,1)} %src_hbm.1, bf16[48,256,128]{2,1,0:T(8,128)(2,1)} %bitcast.4), custom_call_target="tpu_custom_call" | custom-call | flops 150994944 | bytes 3145728 | tf_op jit(solution)/shard_map/pallas_call | solution.py:491
  15.1 0.6 %shard_map.69 = (bf16[3,3,8,256]{3,2,1,0:T(8,128)(2,1)}, bf16[3,3,8,256]{3,2,1,0:T(8,128)(2,1)}) custom-call(bf16[2,3,3,8,256]{4,3,2,1,0:T(8,128)(2,1)S(1)} %shard_map.68.both_ref), custom_call_target="tpu_custom_call" | custom-call | tf_op jit(solution)/shard_map/pallas_call | solution.py:539

commit v4 on v3

--- a/solution.py
+++ b/solution.py
@@ -69,7 +69,9 @@
 
     def key(d):
         hops = d % 2 + d // 2 % 2 + d // quarter
-        return (4 * hops - ((d // quarter - 1) % 4 == 1)) * domains + d
+        shift = (0, 0, -1, 4)
+        moved = sum(shift[p] * (d // quarter == p) for p in range(4))
+        return (4 * hops + moved) * domains + d
 
     def wait_if(condition, sem, value):
         @pl.when(condition)
@@ -212,15 +214,15 @@
         to = me ^ (domains - 1 - i) ^ even
         return jnp.where(plane == 3, to, lower * mid + i)
 
-    def first(i):
+    def first(i, **part):
         to = first_of(i)
         ready(to)
-        across(to)
-
-    def second(i, number=full):
+        across(to, **part)
+
+    def second(i, **part):
         to = me ^ (mid + quarter - 1 - i) ^ even
         ready(to)
-        across(to, number=number)
+        across(to, **part)
 
     def beside(known):
         def send(i):
@@ -241,24 +243,6 @@
     steps(domains, announce)
     pl.when(gives)(twin.start)
     swap.start()
-    pl.when(upper == 0)(lambda: beside(True))
-    steps(quarter, first)
-
-    @pl.when(upper == 1)
-    def _():
-        @pl.when(jnp.logical_not(takes))
-        def _():
-            steps(quarter, second)
-
-        beside(True)
-
-    wait_if(near_before < mid - 1, near_sem, mid - 1 - near_before)
-    beside(False)
-
-    @pl.when((upper == 0) & jnp.logical_not(takes))
-    def _():
-        steps(quarter, second)
-
     def rim_of(i):
         to, lines = lower * mid + i, []
         for j in range(per_owner):
@@ -268,12 +252,36 @@
             lines.append(jnp.zeros((half - full, cells), jnp.float32))
         pack[to * planes + full] = jnp.concatenate(lines, axis=0).astype(jnp.bfloat16)
 
+    early = quarter - 1
+
+    def fork(send, start, number):
+        @pl.when(takes)
+        def _():
+            steps(number, lambda i: send(i + start, number=planes))
+
+        @pl.when(jnp.logical_not(takes))
+        def _():
+            steps(number, lambda i: send(i + start))
+
+    pl.when(upper == 0)(lambda: beside(True))
+    steps(early, first)
+
     @pl.when(takes)
     def _():
         twin.wait_recv()
         steps(mid, rim_of)
-        steps(quarter, lambda i: across(first_of(i), start=full, number=1))
-        steps(quarter, lambda i: second(i, planes))
+        steps(early, lambda i: across(first_of(i), start=full, number=1))
+
+    fork(first, early, quarter - early)
+
+    @pl.when(upper == 1)
+    def _():
+        fork(second, 0, quarter)
+        beside(True)
+
+    wait_if(near_before < mid - 1, near_sem, mid - 1 - near_before)
+    beside(False)
+    pl.when(upper == 0)(lambda: fork(second, 0, quarter))
 
     link = lax.broadcasted_iota(jnp.int32, (link_count, owners), 0)
     mine = []
@@ -393,17 +401,27 @@
         steps(quarter, lambda i: product([far_half(i)]))
         pl.when(core == 0)(early_edge)
 
-    @pl.when(core == 0)
-    def _():
-        steps(quarter, lambda i: arrive(3 + i, full))
-
-    @pl.when(core == 1)
-    def _():
-        steps(quarter, lambda i: arrive(3 + i, planes))
+    def arrive_near(offset):
+        @pl.when(core == 0)
+        def _():
+            arrive(3 + offset, full)
+
+        @pl.when(core == 1)
+        def _():
+            arrive(3 + offset, planes)
+
+    def offset_of(i):
+        by_column = lower * other
+        return by_column * (i ^ (me % quarter)) + (1 - by_column) * (quarter - 1 - i)
 
     if domains <= 16:
-        product([near_half(i) for i in range(quarter)], rimmed=True)
+        for i in range(0, quarter, 2):
+            pair = [offset_of(i), offset_of(i + 1)]
+            for offset in pair:
+                arrive_near(offset)
+            product([near_half(offset) for offset in pair], rimmed=True)
     else:
+        steps(quarter, arrive_near)
         steps(quarter, lambda i: product([near_half(i)], rimmed=True))
 
     total = acc[...].reshape(tiles, comps, half, 2 * width)

time: 15.9 us -> 15.7 us (0.987)
  Pallas kernels: 15.1 us -> 14.9 us
    pallas_call x1, Pallas kernels: 14.5 us -> 14.3 us  [shards(): pl.pallas_call(functools.partial(kernel, domains, per_owner), out_shape=v...]
where the time goes in v4:
time: 15.7 us; the launch traced here: 15.6 us
  Pallas kernels  14.9 us (95%)
  between operations  0.64 us (4%)
    pallas_call x1, Pallas kernels, shards(): pl.pallas_call(functools.partial(kernel, domains, per_owner), out_shape=v...  14.3 us
    pallas_call x1, Pallas kernels, shards(): pl.pallas_call(deliver, out_shape=(out, out), in_specs=[in_vmem], out_spe...  0.65 us

profile of v4, /device:TPU:25, one launch (start us, length us, event | category | flops | bytes accessed | tf_op | source)
XLA Modules:
  0.0 15.6 jit_solution(3342963868128945840)
XLA Ops:
  0.6 14.3 %shard_map.68.both_ref = bf16[2,3,3,8,256]{4,3,2,1,0:T(8,128)(2,1)S(1)} custom-call(s32[1,48]{1,0:T(1,128)} %bitcast.7, s32[1,256]{1,0:T(1,128)} %bitcast.6, s32[16,48]{1,0:T(8,128)} %bitcast.5, bf16[16,3,8,256]{3,2,1,0:T(8,128)(2,1)} %src_hbm.1, bf16[48,256,128]{2,1,0:T(8,128)(2,1)} %bitcast.4), custom_call_target="tpu_custom_call" | custom-call | flops 150994944 | bytes 3145728 | tf_op jit(solution)/shard_map/pallas_call | solution.py:509
  14.9 0.6 %shard_map.69 = (bf16[3,3,8,256]{3,2,1,0:T(8,128)(2,1)}, bf16[3,3,8,256]{3,2,1,0:T(8,128)(2,1)}) custom-call(bf16[2,3,3,8,256]{4,3,2,1,0:T(8,128)(2,1)S(1)} %shard_map.68.both_ref), custom_call_target="tpu_custom_call" | custom-call | tf_op jit(solution)/shard_map/pallas_call | solution.py:557

commit v5 on v4

--- a/solution.py
+++ b/solution.py
@@ -45,9 +45,9 @@
     tile_hbm, row_hbm, cross_hbm, src_hbm, w_hbm, out_ref,
     tile_ref, row_ref, cross_ref, src_ref,
     wide_tile, wide_row, wide_cross, send_to, link_one, link_two,
-    w_ref, pack, buf, acc, edge, beyond, twin_ref, rim_acc,
-    in_sem, w_sem, send_sem, recv_sem, wsend_sem, wrecv_sem, edge_sem, flag_sem, near_sem,
-    twin_sem,
+    w_ref, pack, buf, acc, edge, beyond, twin_ref, rim_acc, rim_out, rim_in,
+    in_sem, w_sem, send_sem, recv_sem, side_sem, wrecv_sem, edge_sem, flag_sem, near_sem,
+    twin_sem, rim_sem,
 ):
     me = lax.axis_index("dom")
     core = lax.axis_index("tm")
@@ -84,7 +84,7 @@
         return 2 + near_from * (1 + offset)
 
     inputs = [
-        pltpu.make_async_copy(source, target, in_sem.at[i])
+        pltpu.make_async_copy(source, target, in_sem.at[i // 3])
         for i, (source, target) in enumerate(
             (
                 (tile_hbm, tile_ref),
@@ -120,7 +120,7 @@
         return pltpu.make_async_remote_copy(
             src_ref=w_hbm,
             dst_ref=w_ref.at[part],
-            send_sem=wsend_sem,
+            send_sem=side_sem,
             recv_sem=wrecv_sem,
             device_id=(me, other),
             device_id_type=mesh_type,
@@ -130,8 +130,8 @@
     twin = pltpu.make_async_remote_copy(
         src_ref=src_hbm,
         dst_ref=twin_ref,
-        send_sem=twin_sem.at[0],
-        recv_sem=twin_sem.at[1],
+        send_sem=side_sem,
+        recv_sem=twin_sem,
         device_id=(me, other),
         device_id_type=mesh_type,
     )
@@ -142,6 +142,8 @@
 
     before, near_before = below(0, domains), below(upper * mid, mid)
 
+    flag = me % quarter + plane % 2 * (quarter - me % quarter)
+
     def announce(i):
         known = key(i) < key(me)
 
@@ -152,7 +154,7 @@
         @pl.when(known & (i // mid != upper))
         def _():
             pl.semaphore_signal(
-                flag_sem.at[me % mid], inc=1, device_id=(i, core), device_id_type=mesh_type
+                flag_sem.at[flag], inc=1, device_id=(i, core), device_id_type=mesh_type
             )
 
     for load in inputs[:3]:
@@ -207,22 +209,17 @@
     def across(to, **part):
         exchange(to, mailbox((me ^ to) % quarter), **part).start()
 
-    def ready(to):
-        wait_if(key(to) > key(me), flag_sem.at[to % mid], 1)
-
     def first_of(i):
         to = me ^ (domains - 1 - i) ^ even
         return jnp.where(plane == 3, to, lower * mid + i)
 
     def first(i, **part):
         to = first_of(i)
-        ready(to)
+        wait_if(key(to) > key(me), flag_sem.at[to % quarter], 1)
         across(to, **part)
 
     def second(i, **part):
-        to = me ^ (mid + quarter - 1 - i) ^ even
-        ready(to)
-        across(to, **part)
+        across(me ^ (mid + quarter - 1 - i) ^ even, **part)
 
     def beside(known):
         def send(i):
@@ -274,14 +271,23 @@
 
     fork(first, early, quarter - early)
 
+    later = lower * mid + quarter
+    due = quarter - below(later, quarter)
+
     @pl.when(upper == 1)
     def _():
+        wait_if(due > 0, flag_sem.at[quarter], due)
         fork(second, 0, quarter)
         beside(True)
 
     wait_if(near_before < mid - 1, near_sem, mid - 1 - near_before)
     beside(False)
-    pl.when(upper == 0)(lambda: fork(second, 0, quarter))
+
+    @pl.when(upper == 0)
+    def _():
+        pl.semaphore_wait(flag_sem.at[quarter], due)
+        fork(second, 0, quarter)
+
 
     link = lax.broadcasted_iota(jnp.int32, (link_count, owners), 0)
     mine = []
@@ -307,15 +313,18 @@
 
     acc[...] = jnp.zeros_like(acc)
 
-    def product(sources, rimmed=False):
+    def product(sources, offsets=None):
+        rimmed = offsets is not None
         totals = [acc[t] for t in range(tiles)]
         outer = [[0.0] * tiles for _ in range(per_owner)]
-        for frm in sources:
+        for k, frm in enumerate(sources):
             for j in range(per_owner):
                 here = buf[pl.ds(frm * planes + j * comps, comps)].astype(jnp.float32)
                 lhs = here.reshape(count, cells)
                 if rimmed:
-                    rim = jnp.where(core == 1, buf[frm * planes + full].astype(jnp.float32), 0.0)
+                    rest = rim_in[offsets[k]].astype(jnp.float32)
+                    rim = buf[frm * planes + full].astype(jnp.float32)
+                    rim = jnp.where(core == 1, rim, rest)
                     lhs = jnp.concatenate([lhs, rim], axis=0)
                 lhs = lhs.astype(jnp.bfloat16)
                 one = link_one[frm * per_owner + j]
@@ -373,15 +382,15 @@
     halo = pltpu.make_async_remote_copy(
         src_ref=edge,
         dst_ref=beyond,
-        send_sem=edge_sem.at[0],
-        recv_sem=edge_sem.at[1],
+        send_sem=side_sem,
+        recv_sem=edge_sem,
         device_id=(me, other),
         device_id_type=mesh_type,
     )
 
     def early_edge():
         now = acc[...].reshape(tiles, comps, half, 2 * width)
-        edge[...] = now[:, :, half - 1]
+        edge[...] = jnp.where(core == 0, now[:, :, half - 1], now[:, :, 0])
         halo.start()
 
     if domains <= 16:
@@ -392,14 +401,14 @@
         product([jnp.where(plane == 0, far_half(i), own_half(i)) for i in range(quarter)])
         arrive(2 - outmost, quarter * full)
         product([jnp.where(plane == 0, own_half(i), far_half(i)) for i in range(quarter)])
-        pl.when(core == 0)(early_edge)
+        early_edge()
     else:
         arrive(0, (quarter - 1) * full)
         arrive(1, quarter * full)
         arrive(2, quarter * full)
         steps(mid, lambda r: product([me ^ r]))
         steps(quarter, lambda i: product([far_half(i)]))
-        pl.when(core == 0)(early_edge)
+        early_edge()
 
     def arrive_near(offset):
         @pl.when(core == 0)
@@ -414,22 +423,43 @@
         by_column = lower * other
         return by_column * (i ^ (me % quarter)) + (1 - by_column) * (quarter - 1 - i)
 
-    if domains <= 16:
-        for i in range(0, quarter, 2):
-            pair = [offset_of(i), offset_of(i + 1)]
+    def handed(base):
+        return pltpu.make_async_remote_copy(
+            src_ref=rim_out.at[pl.ds(base, 2)],
+            dst_ref=rim_in.at[pl.ds(base, 2)],
+            send_sem=side_sem,
+            recv_sem=rim_sem.at[base // 2],
+            device_id=(me, other),
+            device_id_type=mesh_type,
+        )
+
+    def hand(offset):
+        frm, lines = near_half(offset), []
+        for j in range(per_owner):
+            block = buf[pl.ds(frm * planes + j * comps, comps)].astype(jnp.float32)
+            lines.append(block[:, 0])
+        if half > full:
+            lines.append(jnp.zeros((half - full, cells), jnp.float32))
+        rim_out[offset] = jnp.concatenate(lines, axis=0).astype(jnp.bfloat16)
+
+    def late(i):
+        pair = [offset_of(i), offset_of(i + 1)]
+        base = pair[0] // 2 * 2
+        for offset in pair:
+            arrive_near(offset)
+
+        @pl.when(core == 1)
+        def _():
             for offset in pair:
-                arrive_near(offset)
-            product([near_half(offset) for offset in pair], rimmed=True)
-    else:
-        steps(quarter, arrive_near)
-        steps(quarter, lambda i: product([near_half(i)], rimmed=True))
+                hand(offset)
+            handed(base).start()
+
+        pl.when(core == 0)(handed(base).wait_recv)
+        product([near_half(offset) for offset in pair], pair)
+
+    steps(quarter // 2, lambda i: late(2 * i))
 
     total = acc[...].reshape(tiles, comps, half, 2 * width)
-
-    @pl.when(core == 1)
-    def _():
-        edge[...] = total[:, :, 0]
-        halo.start()
 
     out_ref[0] = total.astype(jnp.bfloat16)
 
@@ -452,8 +482,6 @@
     def _():
         drain((domains - 1) * full)
 
-    swap.wait_send()
-    pl.when(gives)(twin.wait_send)
     halo.wait_recv()
     sample = lax.broadcasted_iota(jnp.int32, (half, 2 * width), 0)
     for t in range(tiles):
@@ -473,7 +501,13 @@
                 ),
             )
             out_ref[1, t, p] = rate.astype(jnp.bfloat16)
+    swap.wait_send()
+    pl.when(gives)(twin.wait_send)
     halo.wait_send()
+
+    @pl.when(core == 1)
+    def _():
+        steps(quarter // 2, lambda i: handed(2 * i).wait_send())
 
 
 def deliver(both_ref, source_ref, rate_ref, sem):
@@ -530,16 +564,19 @@
             vmem((tiles, comps, 2 * width), jnp.float32),
             vmem(sources.shape, jnp.bfloat16),
             vmem((tiles, comps, 2 * width), jnp.float32),
-            dma((4,)),
+            vmem((domains // 4,) + block, jnp.bfloat16),
+            vmem((domains // 4,) + block, jnp.bfloat16),
+            dma((2,)),
             dma,
             dma,
             dma((3 + domains // 4,)),
             dma,
             dma,
-            dma((2,)),
-            regular((domains // 2,)),
+            dma,
+            regular((domains // 4 + 1,)),
             regular,
-            dma((2,)),
+            dma,
+            dma((domains // 8,)),
         ],
         compiler_params=pltpu.CompilerParams(collective_id=0, has_side_effects=True),
         cost_estimate=pl.CostEstimate(

time: 15.7 us -> 15.8 us (level)
  the two profiles are of different devices: /device:TPU:25 before, /device:TPU:0 now
where the time goes in v5:
time: 15.8 us; the launch traced here: 15.7 us
  Pallas kernels  15 us (95%)
  between operations  0.64 us (4%)
    pallas_call x1, Pallas kernels, shards(): pl.pallas_call(functools.partial(kernel, domains, per_owner), out_shape=v...  14.4 us
    pallas_call x1, Pallas kernels, shards(): pl.pallas_call(deliver, out_shape=(out, out), in_specs=[in_vmem], out_spe...  0.65 us

profile of v5, /device:TPU:0, one launch (start us, length us, event | category | flops | bytes accessed | tf_op | source)
XLA Modules:
  0.0 15.7 jit_solution(4787521757832471425)
XLA Ops:
  0.6 14.4 %shard_map.68.both_ref = bf16[2,3,3,8,256]{4,3,2,1,0:T(8,128)(2,1)S(1)} custom-call(s32[1,48]{1,0:T(1,128)} %bitcast.7, s32[1,256]{1,0:T(1,128)} %bitcast.6, s32[16,48]{1,0:T(8,128)} %bitcast.5, bf16[16,3,8,256]{3,2,1,0:T(8,128)(2,1)} %src_hbm.1, bf16[48,256,128]{2,1,0:T(8,128)(2,1)} %bitcast.4), custom_call_target="tpu_custom_call" | custom-call | flops 150994944 | bytes 3145728 | tf_op jit(solution)/shard_map/pallas_call | solution.py:543
  15.0 0.6 %shard_map.69 = (bf16[3,3,8,256]{3,2,1,0:T(8,128)(2,1)}, bf16[3,3,8,256]{3,2,1,0:T(8,128)(2,1)}) custom-call(bf16[2,3,3,8,256]{4,3,2,1,0:T(8,128)(2,1)S(1)} %shard_map.68.both_ref), custom_call_target="tpu_custom_call" | custom-call | tf_op jit(solution)/shard_map/pallas_call | solution.py:594

commit v6 on v5

--- a/solution.py
+++ b/solution.py
@@ -249,6 +249,13 @@
             lines.append(jnp.zeros((half - full, cells), jnp.float32))
         pack[to * planes + full] = jnp.concatenate(lines, axis=0).astype(jnp.bfloat16)
 
+    def rim_alone(i):
+        to = first_of(i)
+
+        @pl.when(to > 0)
+        def _():
+            across(to, start=full, number=1)
+
     early = quarter - 1
 
     def fork(send, start, number):
@@ -267,7 +274,7 @@
     def _():
         twin.wait_recv()
         steps(mid, rim_of)
-        steps(early, lambda i: across(first_of(i), start=full, number=1))
+        steps(early, rim_alone)
 
     fork(first, early, quarter - early)
 
@@ -324,7 +331,7 @@
                 if rimmed:
                     rest = rim_in[offsets[k]].astype(jnp.float32)
                     rim = buf[frm * planes + full].astype(jnp.float32)
-                    rim = jnp.where(core == 1, rim, rest)
+                    rim = jnp.where(core == 0, rest, jnp.where(me == 0, 0.0, rim))
                     lhs = jnp.concatenate([lhs, rim], axis=0)
                 lhs = lhs.astype(jnp.bfloat16)
                 one = link_one[frm * per_owner + j]
@@ -388,7 +395,9 @@
         device_id_type=mesh_type,
     )
 
-    def early_edge():
+    tardy = (core == 0) & (me == 0)
+
+    def give_edge():
         now = acc[...].reshape(tiles, comps, half, 2 * width)
         edge[...] = jnp.where(core == 0, now[:, :, half - 1], now[:, :, 0])
         halo.start()
@@ -401,21 +410,23 @@
         product([jnp.where(plane == 0, far_half(i), own_half(i)) for i in range(quarter)])
         arrive(2 - outmost, quarter * full)
         product([jnp.where(plane == 0, own_half(i), far_half(i)) for i in range(quarter)])
-        early_edge()
+        pl.when(jnp.logical_not(tardy))(give_edge)
     else:
         arrive(0, (quarter - 1) * full)
         arrive(1, quarter * full)
         arrive(2, quarter * full)
         steps(mid, lambda r: product([me ^ r]))
         steps(quarter, lambda i: product([far_half(i)]))
-        early_edge()
+        pl.when(jnp.logical_not(tardy))(give_edge)
+
+    bare = (core == 0) | (me == 0)
 
     def arrive_near(offset):
-        @pl.when(core == 0)
+        @pl.when(bare)
         def _():
             arrive(3 + offset, full)
 
-        @pl.when(core == 1)
+        @pl.when(jnp.logical_not(bare))
         def _():
             arrive(3 + offset, planes)
 
@@ -458,6 +469,7 @@
         product([near_half(offset) for offset in pair], pair)
 
     steps(quarter // 2, lambda i: late(2 * i))
+    pl.when(tardy)(give_edge)
 
     total = acc[...].reshape(tiles, comps, half, 2 * width)
 
@@ -474,9 +486,13 @@
             device_id_type=mesh_type,
         ).wait_send()
 
-    @pl.when(takes)
+    @pl.when(takes & (plane == 1))
     def _():
         drain((domains - 1) * full + mid)
+
+    @pl.when(takes & (plane == 2))
+    def _():
+        drain((domains - 1) * full + mid - 1)
 
     @pl.when(jnp.logical_not(takes))
     def _():

time: 15.8 us -> 15.7 us (level)
  the two profiles are of different devices: /device:TPU:0 before, /device:TPU:8 now
where the time goes in v6:
time: 15.7 us; the launch traced here: 15.5 us
  Pallas kernels  14.9 us (95%)
  between operations  0.64 us (4%)
    pallas_call x1, Pallas kernels, shards(): pl.pallas_call(functools.partial(kernel, domains, per_owner), out_shape=v...  14.2 us
    pallas_call x1, Pallas kernels, shards(): pl.pallas_call(deliver, out_shape=(out, out), in_specs=[in_vmem], out_spe...  0.65 us

profile of v6, /device:TPU:8, one launch (start us, length us, event | category | flops | bytes accessed | tf_op | source)
XLA Modules:
  0.0 15.5 jit_solution(14852291142057796609)
XLA Ops:
  0.6 14.2 %shard_map.68.both_ref = bf16[2,3,3,8,256]{4,3,2,1,0:T(8,128)(2,1)S(1)} custom-call(s32[1,48]{1,0:T(1,128)} %bitcast.7, s32[1,256]{1,0:T(1,128)} %bitcast.6, s32[16,48]{1,0:T(8,128)} %bitcast.5, bf16[16,3,8,256]{3,2,1,0:T(8,128)(2,1)} %src_hbm.1, bf16[48,256,128]{2,1,0:T(8,128)(2,1)} %bitcast.4), custom_call_target="tpu_custom_call" | custom-call | flops 150994944 | bytes 3145728 | tf_op jit(solution)/shard_map/pallas_call | solution.py:559
  14.9 0.6 %shard_map.69 = (bf16[3,3,8,256]{3,2,1,0:T(8,128)(2,1)}, bf16[3,3,8,256]{3,2,1,0:T(8,128)(2,1)}) custom-call(bf16[2,3,3,8,256]{4,3,2,1,0:T(8,128)(2,1)S(1)} %shard_map.68.both_ref), custom_call_target="tpu_custom_call" | custom-call | tf_op jit(solution)/shard_map/pallas_call | solution.py:610

commit v7 on v6

--- a/solution.py
+++ b/solution.py
@@ -431,8 +431,7 @@
             arrive(3 + offset, planes)
 
     def offset_of(i):
-        by_column = lower * other
-        return by_column * (i ^ (me % quarter)) + (1 - by_column) * (quarter - 1 - i)
+        return quarter - 1 - i
 
     def handed(base):
         return pltpu.make_async_remote_copy(

time: 15.7 us -> 15.4 us (0.981)
  the two profiles are of different devices: /device:TPU:8 before, /device:TPU:25 now
where the time goes in v7:
time: 15.4 us; the launch traced here: 15.2 us
  Pallas kernels  14.6 us (95%)
  between operations  0.64 us (4%)
    pallas_call x1, Pallas kernels, shards(): pl.pallas_call(functools.partial(kernel, domains, per_owner), out_shape=v...  13.9 us
    pallas_call x1, Pallas kernels, shards(): pl.pallas_call(deliver, out_shape=(out, out), in_specs=[in_vmem], out_spe...  0.65 us

profile of v7, /device:TPU:25, one launch (start us, length us, event | category | flops | bytes accessed | tf_op | source)
XLA Modules:
  0.0 15.2 jit_solution(11091383924346989123)
XLA Ops:
  0.6 13.9 %shard_map.68.both_ref = bf16[2,3,3,8,256]{4,3,2,1,0:T(8,128)(2,1)S(1)} custom-call(s32[1,48]{1,0:T(1,128)} %bitcast.7, s32[1,256]{1,0:T(1,128)} %bitcast.6, s32[16,48]{1,0:T(8,128)} %bitcast.5, bf16[16,3,8,256]{3,2,1,0:T(8,128)(2,1)} %src_hbm.1, bf16[48,256,128]{2,1,0:T(8,128)(2,1)} %bitcast.4), custom_call_target="tpu_custom_call" | custom-call | flops 150994944 | bytes 3145728 | tf_op jit(solution)/shard_map/pallas_call | solution.py:558
  14.6 0.6 %shard_map.69 = (bf16[3,3,8,256]{3,2,1,0:T(8,128)(2,1)}, bf16[3,3,8,256]{3,2,1,0:T(8,128)(2,1)}) custom-call(bf16[2,3,3,8,256]{4,3,2,1,0:T(8,128)(2,1)S(1)} %shard_map.68.both_ref), custom_call_target="tpu_custom_call" | custom-call | tf_op jit(solution)/shard_map/pallas_call | solution.py:609
